TPU v7x, 32 devices: a whole 2x2x4 slice. The times are simulated.
32 devices in a mesh: agent: 4 (over x, core), tp: 8 (over z, y).
Axes of the slice: x: 2, y: 2, z: 4, core: 2. Of those that a mesh axis runs over, the one named last changes fastest.
Arguments:
- tokens: bfloat16 [4, 512, 2048], P('agent', 'tp'), may hold values from -6 to 6
- targets: bfloat16 [4, 512, 2048], P('agent', 'tp'), may hold values from -6 to 6
- params: bfloat16 [4, 2048, 8192], P('agent', None, 'tp'), may hold values from -6 to 6
- tracker: bfloat16 [4, 2048, 8192], P('agent', None, 'tp'), may hold values from -6 to 6
- up_weight: bfloat16 [2048, 8192], P('agent', 'tp'), may hold values from -0.125 to 0.125
- down_weight: bfloat16 [8192, 2048], P('tp', 'agent'), may hold values from -0.0625 to 0.0625
- edge_weight: float32 [4], replicated, may hold values from 0.1 to 0.4
- step_size: float32 [1], replicated, may hold values from 0.1 to 0.5
Outputs:
- new_params: bfloat16 [4, 2048, 8192], P('agent', None, 'tp')
- new_tracker: bfloat16 [4, 2048, 8192], P('agent', None, 'tp')
All inputs are finite; a program needn't handle non-finite values.
Results may differ from a plain program's by a relative error of at most 0.033.
Values may be sent and summed in bfloat16 or wider, within the bound.
No kernel may reach another device: no remote copies, remote signals or barrier semaphores. Data moves between devices by JAX's collectives and lax.ppermute only.
A program may use at most 128 MiB of HBM per device.

v0:
```python
import jax
import jax.numpy as jnp
from jax import lax
from jax.sharding import PartitionSpec as P


def passed_along(value, axis, steps):
    count = lax.axis_size(axis)
    pairs = [(source, (source + steps) % count) for source in range(count)]
    return lax.ppermute(value, axis, pairs)


def on_device(tokens, targets, params, tracker, up_weight, down_weight, edge_weight, step_size):
    target_rows = targets[0]
    param = params[0]
    track = tracker[0]
    left_x, left_y = passed_along((param, track), "agent", 1)
    right_x, right_y = passed_along((param, track), "agent", -1)
    up_full, down_full = (
        lax.all_gather(up_weight, "agent", axis=0, tiled=True),
        lax.all_gather(down_weight, "agent", axis=1, tiled=True),
    )
    whole, whole_targets = (
        lax.all_gather(tokens[0], "tp", axis=0, tiled=True),
        lax.all_gather(target_rows, "tp", axis=0, tiled=True),
    )
    scale = 1.0 / whole.shape[1] ** 0.5
    up = jnp.dot(whole, up_full, preferred_element_type=jnp.float32)

    def dgate_of(weights):
        gate = jnp.dot(whole, weights, preferred_element_type=jnp.float32) * scale
        sig = jax.nn.sigmoid(gate)
        hidden = (sig * gate * up).astype(jnp.bfloat16)
        partial_value = jnp.dot(hidden, down_full, preferred_element_type=jnp.float32)
        summed = lax.psum(partial_value.astype(jnp.bfloat16), "tp").astype(jnp.float32)
        err = (2.0 * (summed - whole_targets.astype(jnp.float32))).astype(jnp.bfloat16)
        back = lax.dot_general(
            err, down_full, (((1,), (1,)), ((), ())), preferred_element_type=jnp.float32
        )
        return (back * up * sig * (1.0 + gate * (1.0 - sig))).astype(jnp.bfloat16)

    def weight_grad(dgate):
        return lax.dot_general(
            whole, dgate, (((0,), (0,)), ((), ())), preferred_element_type=jnp.float32
        )

    old_grad = weight_grad(dgate_of(param))
    count = lax.axis_size("agent")
    index = lax.axis_index("agent")
    e_right = lax.dynamic_slice_in_dim(edge_weight, index, 1)[0]
    e_left = lax.dynamic_slice_in_dim(edge_weight, (index + count - 1) % count, 1)[0]
    own = 1.0 - e_right - e_left
    track32 = track.astype(jnp.float32)
    mixed_x = (
        own * param.astype(jnp.float32)
        + e_right * right_x.astype(jnp.float32)
        + e_left * left_x.astype(jnp.float32)
    )
    mixed_y = (
        own * track32 + e_right * right_y.astype(jnp.float32) + e_left * left_y.astype(jnp.float32)
    )
    fresh = (mixed_x - step_size[0] * track32).astype(jnp.bfloat16)
    new_grad = weight_grad(dgate_of(fresh))
    fresh_track = (mixed_y + (new_grad - old_grad) * scale).astype(jnp.bfloat16)
    return (fresh[None], fresh_track[None])


def solution(mesh):
    return jax.shard_map(
        on_device,
        mesh=mesh,
        in_specs=(
            P("agent", "tp", None),
            P("agent", "tp", None),
            P("agent", None, "tp"),
            P("agent", None, "tp"),
            P("agent", "tp"),
            P("tp", "agent"),
            P(),
            P(),
        ),
        out_specs=(P("agent", None, "tp"), P("agent", None, "tp")),
        check_vma=False,
    )
```

profile of v0, /device:TPU:0, one launch (start us, length us, event | category | flops | bytes accessed | tf_op | source)
XLA Modules:
  0.0 413.9 jit_solution(9907880872152286384)
XLA Ops:
  7.2 0.0 all-gather.11.cloned.1.call-start
  7.2 0.7 all-gather.11.cloned.1.call-update
  7.9 0.0 all-gather.7.cloned.1.call-start
  7.9 0.7 all-gather.7.cloned.1.call-update
  8.6 0.0 all-gather.9.cloned.1.call-start
  8.7 0.7 all-gather.9.cloned.1.call-update
  9.4 0.0 all-gather.13.cloned.1.call-start
  9.4 6.4 %copy.10 = bf16[1,2048,1024]{1,2,0:T(8,128)(2,1)} copy(bf16[1,2048,1024]{2,1,0:T(8,128)(2,1)} %param.10) | data formatting | bytes 8388608 | tf_op args[2]
  15.9 2.4 collective-permute-start
  18.3 0.0 collective-permute-start.1
  18.3 0.0 all-gather.13.cloned.1.call-update
  18.3 0.0 all-reduce.3.cloned.1.call-start
  19.0 0.0 copy-start.3
  19.0 6.6 %copy.11 = bf16[1,2048,1024]{1,2,0:T(8,128)(2,1)} copy(bf16[1,2048,1024]{2,1,0:T(8,128)(2,1)} %param.11) | data formatting | bytes 8388608 | tf_op args[3]
  25.6 0.0 copy-done.3
  25.6 0.6 fusion.62
  27.4 34.6 %all-gather.11.cloned.1.call-done = bf16[1,512,2048]{2,1,0:T(8,128)(2,1)} async-done(((bf16[1,64,2048]{2,1,0:T(8,128)(2,1)}), bf16[1,512,2048]{2,1,0:T(8,128)(2,1)}) %all-gather.11.cloned.1.call-update) | async-done | bytes 2097168 | tf_op jit(solution)/shard_map/all_gather | solution.py:24
  61.9 0.0 copy-start
  61.9 0.0 copy-start.1
  61.9 6.7 %fusion.11 = f32[512,1024]{0,1:T(8,128)} fusion(bf16[1,2048,1024]{2,1,0:T(8,128)(2,1)} %param.10, bf16[1,512,2048]{2,1,0:T(8,128)(2,1)} %all-gather.11.cloned.1.call-done), kind=kOutput, calls=%fused_computation.15 | convolution fusion | flops 2147483648 | bytes 8388608 | tf_op jit(solution)/shard_map/dot_general | solution.py:31
  68.6 66.4 %collective-permute-done = bf16[2048,1024]{0,1:T(8,128)(2,1)} collective-permute-done((bf16[2048,1024]{0,1:T(8,128)(2,1)}, bf16[2048,1024]{0,1:T(8,128)(2,1)}, u32[]{:S(2)}, u32[]{:S(2)}) %collective-permute-start) | collective-permute-done | bytes 4194336 | tf_op jit(solution)/shard_map/ppermute | solution.py:10
  135.0 0.7 collective-permute-done.1
  135.7 0.0 copy-done
  135.7 0.0 copy-done.1
  135.7 0.0 copy-start.5
  135.8 7.8 %fusion.1 = bf16[2048,1024]{0,1:T(8,128)(2,1)S(1)} fusion(bf16[2048,1024]{0,1:T(8,128)(2,1)} %collective-permute-done.1, bf16[2048,1024]{0,1:T(8,128)(2,1)} %collective-permute-done, f32[]{:T(128)} %bitcast.80, f32[]{:T(128)} %bitcast.1, f32[]{:T(128)} %bitcast, f32[]{:T(128)S(6)} %sub.30, bf16[1,2048,1024]{1,2,0:T(8,128)(2,1)S(1)} %copy-done, ...), kind=kLoop, calls=%fused_computation.3 | loop fusion | flops 25165824 | bytes 20971536 | tf_op jit(solution)/shard_map/convert_element_type | solution.py:62
  143.5 0.0 copy-start.2
  143.5 2.0 copy-done.2
  145.5 0.0 copy-done.5
  145.6 3.7 fusion.33
  149.2 0.0 all-gather.7.cloned.1.call-done
  149.2 5.9 %fusion.31 = f32[512,1024]{0,1:T(8,128)} fusion(bf16[2048,1024]{1,0:T(8,128)(2,1)} %all-gather.7.cloned.1.call-done, bf16[1,512,2048]{2,1,0:T(8,128)(2,1)S(1)} %copy-done.5), kind=kOutput, calls=%fused_computation.38 | convolution fusion | flops 2147483648 | bytes 8388608 | tf_op jit(solution)/shard_map/dot_general | solution.py:28
  155.1 1.9 all-gather.9.cloned.1.call-done
  157.0 0.0 copy-start.4
  157.0 0.0 copy-start.6
  157.0 0.0 copy-start.7
  157.0 7.5 %convolution_convert_fusion = bf16[512,2048]{1,0:T(8,128)(2,1)} fusion(bf16[1024,2048]{1,0:T(8,128)(2,1)} %all-gather.9.cloned.1.call-done, f32[512,1024]{0,1:T(8,128)} %fusion.31, f32[512,1024]{0,1:T(8,128)} %fusion.11), kind=kOutput, calls=%fused_computation.17 | convolution fusion | flops 2152202240 | bytes 10485760 | tf_op jit(solution)/shard_map/dot_general | solution.py:34
  164.5 0.0 copy-done.4
  164.5 0.0 copy-done.6
  164.5 0.0 copy-done.7
  164.5 3.9 convolution_convert_fusion.1
  168.5 0.0 all-reduce.3.cloned.1.call-update
  168.5 1.3 collective-permute-start.2
  169.9 0.0 collective-permute-start.3
  169.9 6.4 %copy.17 = bf16[1,2048,1024]{2,1,0:T(8,128)(2,1)} copy(bf16[1,2048,1024]{1,2,0:T(8,128)(2,1)} %bitcast.85) | data formatting | bytes 8388608
  176.3 33.1 %all-gather.13.cloned.1.call-done = bf16[1,512,2048]{2,1,0:T(8,128)(2,1)} async-done(((bf16[1,64,2048]{2,1,0:T(8,128)(2,1)}), bf16[1,512,2048]{2,1,0:T(8,128)(2,1)}) %all-gather.13.cloned.1.call-update) | async-done | bytes 2097168 | tf_op jit(solution)/shard_map/all_gather | solution.py:25
  209.3 158.6 %all-reduce.3.cloned.1.call-done = (bf16[512,2048]{1,0:T(8,128)(2,1)}, bf16[512,2048]{1,0:T(8,128)(2,1)}) async-done(((bf16[512,2048]{1,0:T(8,128)(2,1)}, bf16[512,2048]{1,0:T(8,128)(2,1)}), (bf16[512,2048]{1,0:T(8,128)(2,1)}, bf16[512,2048]{1,0:T(8,128)(2,1)})) %all-reduce.3.cloned.1.call-update) | async-done | bytes 4194320 | tf_op jit(solution)/shard_map/psum | solution.py:35
  367.9 12.9 %fusion.29 = f32[1024,2048]{1,0:T(8,128)} fusion(bf16[1,512,2048]{2,1,0:T(8,128)(2,1)S(1)} %copy-done.5, f32[512,1024]{0,1:T(8,128)} %fusion.31, f32[1024,512]{1,0:T(8,128)} %fusion.33, bf16[1024,2048]{1,0:T(8,128)(2,1)} %all-gather.9.cloned.1.call-done, bf16[512,2048]{1,0:T(8,128)(2,1)} %get-tuple-element.4, ...), kind=kOutput, calls=%fused_computation.36 | convolution fusion | flops 4305977344 | bytes 23068672 | tf_op jit(solution)/shard_map/dot_general | solution.py:43
  380.8 0.0 collective-permute-done.2
  380.8 0.0 collective-permute-done.3
  380.8 20.2 %fusion.10 = bf16[1,2048,1024]{1,2,0:T(8,128)(2,1)} fusion(f32[1024,2048]{1,0:T(8,128)} %fusion.29, bf16[2048,1024]{0,1:T(8,128)(2,1)} %collective-permute-done.3, bf16[2048,1024]{0,1:T(8,128)(2,1)} %collective-permute-done.2, f32[]{:T(128)} %bitcast.1, f32[]{:T(128)} %bitcast, f32[]{:T(128)S(6)} %sub.30, bf16[1,512,2048]{2,1,0:T(8,128)(2,1)S(1)} %copy-done.5, ...), kind=kOutput, calls=%fused_computation.14 | convolution fusion | flops 4331143168 | bytes 39845900 | tf_op jit(solution)/shard_map/dot_general | solution.py:43
  401.0 6.4 %copy.18 = bf16[1,2048,1024]{2,1,0:T(8,128)(2,1)} copy(bf16[1,2048,1024]{1,2,0:T(8,128)(2,1)} %fusion.10) | data formatting | bytes 8388608
Async XLA Ops:
  7.2 54.8 %all-gather.11.cloned.1.call-start = ((), (), s32[]{:S(2)}) async-start(), calls=%async_computation.2 | async-start | bytes 2359296 | tf_op jit(solution)/shard_map/all_gather | solution.py:24
  7.9 141.3 %all-gather.7.cloned.1.call-start = ((), (), s32[]{:S(2)}) async-start(), calls=%async_computation | async-start | bytes 5242880 | tf_op jit(solution)/shard_map/all_gather | solution.py:20
  8.6 148.4 %all-gather.9.cloned.1.call-start = ((), (), s32[]{:S(2)}) async-start(), calls=%async_computation.1 | async-start | bytes 5242880 | tf_op jit(solution)/shard_map/all_gather | solution.py:21
  9.4 199.9 %all-gather.13.cloned.1.call-start = ((), (), s32[]{:S(2)}) async-start(), calls=%async_computation.3 | async-start | bytes 2359296 | tf_op jit(solution)/shard_map/all_gather | solution.py:25
  15.9 119.1 %collective-permute-start = (bf16[2048,1024]{0,1:T(8,128)(2,1)}, bf16[2048,1024]{0,1:T(8,128)(2,1)}, u32[]{:S(2)}, u32[]{:S(2)}) collective-permute-start(bf16[2048,1024]{0,1:T(8,128)(2,1)} %bitcast.83), channel_id=1, source_target_pairs={{0,24},{8,0},{16,8},{24,16},{1,25},{9,1},{17,9},{25,17},{2,26},{10... | collective-permute-start | bytes 12582920 | tf_op jit(solution)/shard_map/ppermute | solution.py:10
  18.3 117.5 %collective-permute-start.1 = (bf16[2048,1024]{0,1:T(8,128)(2,1)}, bf16[2048,1024]{0,1:T(8,128)(2,1)}, u32[]{:S(2)}, u32[]{:S(2)}) collective-permute-start(bf16[2048,1024]{0,1:T(8,128)(2,1)} %bitcast.84), channel_id=1, source_target_pairs={{0,8},{8,16},{16,24},{24,0},{1,9},{9,17},{17,25},{25,1},{2,10},{10... | collective-permute-start | bytes 12582920 | tf_op jit(solution)/shard_map/ppermute | solution.py:10
  18.3 349.6 %all-reduce.3.cloned.1.call-start = ((), (), s32[]{:S(2)}) async-start(), calls=%async_computation.4 | async-start | bytes 8388608 | tf_op jit(solution)/shard_map/psum | solution.py:35
  19.0 6.6 %copy-start.3 = (f32[4]{0:T(128)S(1)}, f32[4]{0:T(128)}, u32[]{:S(2)}) copy-start(f32[4]{0:T(128)} %param.14) | copy-start | bytes 52
  61.9 73.8 %copy-start = (bf16[1,2048,1024]{1,2,0:T(8,128)(2,1)S(1)}, bf16[1,2048,1024]{1,2,0:T(8,128)(2,1)}, u32[]{:S(2)}) copy-start(bf16[1,2048,1024]{1,2,0:T(8,128)(2,1)} %copy.11) | copy-start | bytes 12582916
  61.9 73.8 %copy-start.1 = (bf16[1,2048,1024]{1,2,0:T(8,128)(2,1)S(1)}, bf16[1,2048,1024]{1,2,0:T(8,128)(2,1)}, u32[]{:S(2)}) copy-start(bf16[1,2048,1024]{1,2,0:T(8,128)(2,1)} %copy.10) | copy-start | bytes 12582916
  135.7 9.8 %copy-start.5 = (bf16[1,512,2048]{2,1,0:T(8,128)(2,1)S(1)}, bf16[1,512,2048]{2,1,0:T(8,128)(2,1)}, u32[]{:S(2)}) copy-start(bf16[1,512,2048]{2,1,0:T(8,128)(2,1)} %all-gather.11.cloned.1.call-done) | copy-start | bytes 6291460
  143.5 2.0 copy-start.2
  157.0 7.5 %copy-start.4 = (bf16[1024,2048]{1,0:T(8,128)(2,1)S(1)}, bf16[1024,2048]{1,0:T(8,128)(2,1)}, u32[]{:S(2)}) copy-start(bf16[1024,2048]{1,0:T(8,128)(2,1)} %all-gather.9.cloned.1.call-done) | copy-start | bytes 12582916
  157.0 7.5 %copy-start.6 = (f32[512,1024]{0,1:T(8,128)S(1)}, f32[512,1024]{0,1:T(8,128)}, u32[]{:S(2)}) copy-start(f32[512,1024]{0,1:T(8,128)} %fusion.31) | copy-start | bytes 6291460
  157.0 7.5 %copy-start.7 = (f32[1024,512]{1,0:T(8,128)S(1)}, f32[1024,512]{1,0:T(8,128)}, u32[]{:S(2)}) copy-start(f32[1024,512]{1,0:T(8,128)} %fusion.33) | copy-start | bytes 6291460
  168.5 212.3 %collective-permute-start.2 = (bf16[2048,1024]{0,1:T(8,128)(2,1)}, bf16[2048,1024]{0,1:T(8,128)(2,1)}, u32[]{:S(2)}, u32[]{:S(2)}) collective-permute-start(bf16[2048,1024]{0,1:T(8,128)(2,1)} %bitcast.81), channel_id=1, source_target_pairs={{0,24},{8,0},{16,8},{24,16},{1,25},{9,1},{17,9},{25,17},{2,26},{10... | collective-permute-start | bytes 12582920 | tf_op jit(solution)/shard_map/ppermute | solution.py:10
  169.9 211.0 %collective-permute-start.3 = (bf16[2048,1024]{0,1:T(8,128)(2,1)}, bf16[2048,1024]{0,1:T(8,128)(2,1)}, u32[]{:S(2)}, u32[]{:S(2)}) collective-permute-start(bf16[2048,1024]{0,1:T(8,128)(2,1)} %bitcast.82), channel_id=1, source_target_pairs={{0,8},{8,16},{16,24},{24,0},{1,9},{9,17},{17,25},{25,1},{2,10},{10... | collective-permute-start | bytes 12582920 | tf_op jit(solution)/shard_map/ppermute | solution.py:10
Sparse Core Ops, SparseCore 0:
  10.1 51.7 all-gather.10
  63.5 55.5 all-gather.6
  120.7 36.3 all-gather.8
  159.0 50.2 all-gather.12
  212.9 154.9 all-reduce.2
where the time goes:
time: 415 us; the launch traced here: 414 us
  waiting for transfers between devices  297 us (72%)
  matrix products  60.8 us (15%)
  local copies, waits for them, and re-layouts  28.5 us (7%)
  between operations  15.6 us (4%)
  other arithmetic  7.77 us (2%)
    psum x1, waiting for transfers between devices, dgate_of(): lax.psum(partial_value.astype(jnp.bfloat16), 'tp').astype(jnp.float32)  159 us
    ppermute x4, waiting for transfers between devices, passed_along(): return lax.ppermute(value, axis, pairs)  67.1 us
    all_gather x1, waiting for transfers between devices, on_device(): lax.all_gather(tokens[0], 'tp', axis=0, tiled=True)  34.6 us
    dot_general x2, matrix products, weight_grad(): lax.dot_general(whole, dgate, (((0,), (0,)), ((), ())), preferred_element...  33.1 us
    all_gather x1, waiting for transfers between devices, on_device(): lax.all_gather(target_rows, 'tp', axis=0, tiled=True)  33.1 us
    unnamed x20, local copies, waits for them, and re-layouts  27.9 us
    dot_general x2, matrix products, dgate_of(): jnp.dot(hidden, down_full, preferred_element_type=jnp.float32)  11.5 us
    dot_general x2, matrix products, dgate_of(): gate = jnp.dot(whole, weights, preferred_element_type=jnp.float32) * scale  10.3 us
  transfers between devices with their start and end apart: 9, of which 6 were waited for; matrix products, arithmetic and copies ran while one was open for 17% of the time, Pallas kernels for 0%

commit v1 on v0

--- a/solution.py
+++ b/solution.py
@@ -32,7 +32,9 @@
         sig = jax.nn.sigmoid(gate)
         hidden = (sig * gate * up).astype(jnp.bfloat16)
         partial_value = jnp.dot(hidden, down_full, preferred_element_type=jnp.float32)
-        summed = lax.psum(partial_value.astype(jnp.bfloat16), "tp").astype(jnp.float32)
+        summed = jnp.sum(lax.all_gather(partial_value.astype(jnp.bfloat16), "tp"), axis=0).astype(
+            jnp.float32
+        )
         err = (2.0 * (summed - whole_targets.astype(jnp.float32))).astype(jnp.bfloat16)
         back = lax.dot_general(
             err, down_full, (((1,), (1,)), ((), ())), preferred_element_type=jnp.float32

time: 415 us -> 690 us (1.66)
  waiting for transfers between devices: 297 us -> 554 us
  other arithmetic: 7.77 us -> 30.1 us
    all_gather x0 -> x2, waiting for transfers between devices: none -> 319 us  [dgate_of(): lax.all_gather(partial_value.astype(jnp.bfloat16), 'tp')]
    psum x1 -> x0, waiting for transfers between devices: 159 us -> none  [dgate_of(): lax.psum(partial_value.astype(jnp.bfloat16), 'tp').astype(jnp.float32)]
    all_gather x1, waiting for transfers between devices: 1.89 us -> 30.1 us  [on_device(): lax.all_gather(down_weight, 'agent', axis=1, tiled=True)]
    all_gather x1, waiting for transfers between devices: 0.01 us -> 27.9 us  [on_device(): lax.all_gather(up_weight, 'agent', axis=0, tiled=True)]
    reduce_sum x0 -> x2, other arithmetic: none -> 20.8 us  [dgate_of(): jnp.sum(lax.all_gather(partial_value.astype(jnp.bfloat16), 'tp'), axis=0)]
    all_gather x1, waiting for transfers between devices: 34.6 us -> 52.5 us  [on_device(): lax.all_gather(tokens[0], 'tp', axis=0, tiled=True)]
    ppermute x4, waiting for transfers between devices: 67.1 us -> 83.2 us  [passed_along(): return lax.ppermute(value, axis, pairs)]
    unnamed x20 -> x16, local copies, waits for them, and re-layouts: 27.9 us -> 28.8 us
  transfers between devices with their start and end apart: 9 -> 10, of which waited for: 6 -> 8; matrix products, arithmetic and copies ran while one was open for 17% -> 12% of each run, Pallas kernels for 0% -> 0%
where the time goes in v1:
time: 690 us; the launch traced here: 689 us
  waiting for transfers between devices  554 us (80%)
  matrix products  58.2 us (8%)
  other arithmetic  30.1 us (4%)
  local copies, waits for them, and re-layouts  29.5 us (4%)
  between operations  16.1 us (2%)
    all_gather x2, waiting for transfers between devices, dgate_of(): lax.all_gather(partial_value.astype(jnp.bfloat16), 'tp')  319 us
    ppermute x4, waiting for transfers between devices, passed_along(): return lax.ppermute(value, axis, pairs)  83.2 us
    all_gather x1, waiting for transfers between devices, on_device(): lax.all_gather(tokens[0], 'tp', axis=0, tiled=True)  52.5 us
    all_gather x1, waiting for transfers between devices, on_device(): lax.all_gather(target_rows, 'tp', axis=0, tiled=True)  38.4 us
    dot_general x2, matrix products, weight_grad(): lax.dot_general(whole, dgate, (((0,), (0,)), ((), ())), preferred_element...  31.7 us
    all_gather x1, waiting for transfers between devices, on_device(): lax.all_gather(down_weight, 'agent', axis=1, tiled=True)  30.1 us
    unnamed x16, local copies, waits for them, and re-layouts  28.8 us
    all_gather x1, waiting for transfers between devices, on_device(): lax.all_gather(up_weight, 'agent', axis=0, tiled=True)  27.9 us
  transfers between devices with their start and end apart: 10, of which 8 were waited for; matrix products, arithmetic and copies ran while one was open for 12% of the time, Pallas kernels for 0%

profile of v1, /device:TPU:0, one launch (start us, length us, event | category | flops | bytes accessed | tf_op | source)
XLA Modules:
  0.0 689.2 jit_solution(526174336375646592)
XLA Ops:
  7.2 0.0 all-gather.15.cloned.1.call-start
  7.2 0.7 all-gather.15.cloned.1.call-update
  7.9 0.0 all-gather.11.cloned.1.call-start
  7.9 0.7 all-gather.11.cloned.1.call-update
  8.6 0.0 all-gather.13.cloned.1.call-start
  8.7 0.7 all-gather.13.cloned.1.call-update
  9.4 0.0 all-gather.21.cloned.1.call-start
  9.4 52.5 %all-gather.15.cloned.1.call-done = bf16[1,512,2048]{2,1,0:T(8,128)(2,1)} async-done(((bf16[1,64,2048]{2,1,0:T(8,128)(2,1)}), bf16[1,512,2048]{2,1,0:T(8,128)(2,1)}) %all-gather.15.cloned.1.call-update) | async-done | bytes 2097168 | tf_op jit(solution)/shard_map/all_gather | solution.py:24
  61.9 0.0 copy-start.3
  61.9 6.7 fusion.11
  68.6 27.9 %all-gather.11.cloned.1.call-done = bf16[2048,1024]{1,0:T(8,128)(2,1)} async-done(((bf16[512,1024]{1,0:T(8,128)(2,1)}), bf16[2048,1024]{1,0:T(8,128)(2,1)}) %all-gather.11.cloned.1.call-update) | async-done | bytes 4194320 | tf_op jit(solution)/shard_map/all_gather | solution.py:20
  96.5 0.0 copy-done.3
  96.5 6.0 fusion.31
  102.5 30.1 %all-gather.13.cloned.1.call-done = bf16[1024,2048]{1,0:T(8,128)(2,1)} async-done(((bf16[1024,512]{1,0:T(8,128)(2,1)}), bf16[1024,2048]{1,0:T(8,128)(2,1)}) %all-gather.13.cloned.1.call-update) | async-done | bytes 4194320 | tf_op jit(solution)/shard_map/all_gather | solution.py:21
  132.6 7.4 %convolution_convert_fusion = bf16[512,2048]{1,0:T(8,128)(2,1)} fusion(bf16[1024,2048]{1,0:T(8,128)(2,1)} %all-gather.13.cloned.1.call-done, f32[512,1024]{0,1:T(8,128)} %fusion.31, f32[512,1024]{0,1:T(8,128)} %fusion.11), kind=kOutput, calls=%fused_computation.17 | convolution fusion | flops 2152202240 | bytes 10485760 | tf_op jit(solution)/shard_map/dot_general | solution.py:34
  140.0 0.0 all-gather.21.cloned.1.call-update
  140.0 0.0 all-gather.17.cloned.1.call-start
  140.1 6.4 copy.10
  146.5 0.2 collective-permute-start
  146.7 0.3 collective-permute-start.1
  147.7 0.0 copy-start.1
  147.7 6.8 copy.11
  154.5 0.0 copy-done.1
  154.5 0.7 fusion.62
  156.5 80.4 %collective-permute-done = bf16[2048,1024]{0,1:T(8,128)(2,1)} collective-permute-done((bf16[2048,1024]{0,1:T(8,128)(2,1)}, bf16[2048,1024]{0,1:T(8,128)(2,1)}, u32[]{:S(2)}, u32[]{:S(2)}) %collective-permute-start) | collective-permute-done | bytes 4194336 | tf_op jit(solution)/shard_map/ppermute | solution.py:10
  236.9 2.8 collective-permute-done.1
  239.7 9.2 %fusion.1 = bf16[2048,1024]{0,1:T(8,128)(2,1)S(1)} fusion(bf16[2048,1024]{0,1:T(8,128)(2,1)} %collective-permute-done.1, bf16[2048,1024]{0,1:T(8,128)(2,1)} %collective-permute-done, f32[]{:T(128)} %bitcast.82, f32[]{:T(128)} %bitcast.1, f32[]{:T(128)} %bitcast, f32[]{:T(128)S(6)} %sub.30, bf16[1,2048,1024]{1,2,0:T(8,128)(2,1)} %copy.11, ...), kind=kLoop, calls=%fused_computation.3 | loop fusion | flops 25165824 | bytes 20971536 | tf_op jit(solution)/shard_map/convert_element_type | solution.py:64
  248.9 0.0 copy-start
  248.9 0.0 copy-start.2
  249.0 0.0 copy-start.4
  249.0 2.4 fusion.33
  251.4 0.0 copy-done
  251.4 0.0 copy-start.5
  251.4 1.3 copy-done.5
  252.7 0.7 copy-done.2
  253.4 0.7 copy-done.4
  254.1 4.0 convolution_convert_fusion.1
  258.1 0.0 all-gather.17.cloned.1.call-update
  258.1 0.0 all-gather.19.cloned.1.call-start
  258.1 0.5 all-gather.19.cloned.1.call-update
  258.7 0.1 collective-permute-start.2
  258.7 0.6 collective-permute-start.3
  259.4 6.4 copy.17
  265.7 101.7 %all-gather.21.cloned.1.call-done = bf16[4096,2048]{1,0:T(8,128)(2,1)} async-done(((bf16[512,2048]{1,0:T(8,128)(2,1)}), bf16[4096,2048]{1,0:T(8,128)(2,1)}) %all-gather.21.cloned.1.call-update) | async-done | bytes 16777232 | tf_op jit(solution)/shard_map/all_gather | solution.py:35
  367.5 10.0 %reduce_sum.25 = bf16[512,2048]{1,0:T(8,128)(2,1)S(1)} reduce(bf16[8,512,2048]{2,1,0:T(8,128)(2,1)} %bitcast.83, bf16[]{:T(256)} %constant.32.clone.1), dimensions={0}, to_apply=%region_1.2 | reduce | flops 7340032 | bytes 18874370 | tf_op jit(solution)/shard_map/reduce_sum | solution.py:35
  377.4 217.5 %all-gather.17.cloned.1.call-done = bf16[4096,2048]{1,0:T(8,128)(2,1)} async-done(((bf16[512,2048]{1,0:T(8,128)(2,1)}), bf16[4096,2048]{1,0:T(8,128)(2,1)}) %all-gather.17.cloned.1.call-update) | async-done | bytes 16777232 | tf_op jit(solution)/shard_map/all_gather | solution.py:35
  594.9 10.8 %reduce_sum.24 = bf16[512,2048]{1,0:T(8,128)(2,1)} reduce(bf16[8,512,2048]{2,1,0:T(8,128)(2,1)} %bitcast.84, bf16[]{:T(256)} %constant.32.clone.1), dimensions={0}, to_apply=%region_0.0 | reduce | flops 7340032 | bytes 18874370 | tf_op jit(solution)/shard_map/reduce_sum | solution.py:35
  605.8 38.4 %all-gather.19.cloned.1.call-done = bf16[1,512,2048]{2,1,0:T(8,128)(2,1)} async-done(((bf16[1,64,2048]{2,1,0:T(8,128)(2,1)}), bf16[1,512,2048]{2,1,0:T(8,128)(2,1)}) %all-gather.19.cloned.1.call-update) | async-done | bytes 2097168 | tf_op jit(solution)/shard_map/all_gather | solution.py:25
  644.2 13.5 %fusion.29 = f32[1024,2048]{1,0:T(8,128)} fusion(bf16[1,512,2048]{2,1,0:T(8,128)(2,1)} %all-gather.15.cloned.1.call-done, f32[512,1024]{0,1:T(8,128)} %fusion.31, f32[1024,512]{1,0:T(8,128)} %copy-done.5, bf16[1024,2048]{1,0:T(8,128)(2,1)} %all-gather.13.cloned.1.call-done, bf16[512,2048]{1,0:T(8,128)(2,1)} %reduce_sum.24, ...), kind=kOutput, calls=%fused_computation.36 | convolution fusion | flops 4305977344 | bytes 23068672 | tf_op jit(solution)/shard_map/dot_general | solution.py:45
  657.8 0.0 collective-permute-done.2
  657.8 0.0 collective-permute-done.3
  657.8 18.2 %fusion.10 = bf16[1,2048,1024]{1,2,0:T(8,128)(2,1)} fusion(f32[1024,2048]{1,0:T(8,128)} %fusion.29, bf16[2048,1024]{0,1:T(8,128)(2,1)} %collective-permute-done.3, bf16[2048,1024]{0,1:T(8,128)(2,1)} %collective-permute-done.2, f32[]{:T(128)} %bitcast.1, f32[]{:T(128)} %bitcast, f32[]{:T(128)S(6)} %sub.30, ...), kind=kOutput, calls=%fused_computation.14 | convolution fusion | flops 4331143168 | bytes 39845900 | tf_op jit(solution)/shard_map/dot_general | solution.py:45
  676.0 6.4 copy.18
Async XLA Ops:
  7.2 54.8 %all-gather.15.cloned.1.call-start = ((), (), s32[]{:S(2)}) async-start(), calls=%async_computation.2 | async-start | bytes 2359296 | tf_op jit(solution)/shard_map/all_gather | solution.py:24
  7.9 88.6 %all-gather.11.cloned.1.call-start = ((), (), s32[]{:S(2)}) async-start(), calls=%async_computation | async-start | bytes 5242880 | tf_op jit(solution)/shard_map/all_gather | solution.py:20
  8.6 123.9 %all-gather.13.cloned.1.call-start = ((), (), s32[]{:S(2)}) async-start(), calls=%async_computation.1 | async-start | bytes 5242880 | tf_op jit(solution)/shard_map/all_gather | solution.py:21
  9.4 358.1 %all-gather.21.cloned.1.call-start = ((), (), s32[]{:S(2)}) async-start(), calls=%async_computation.5 | async-start | bytes 18874368 | tf_op jit(solution)/shard_map/all_gather | solution.py:35
  61.9 34.6 %copy-start.3 = (bf16[1,512,2048]{2,1,0:T(8,128)(2,1)S(1)}, bf16[1,512,2048]{2,1,0:T(8,128)(2,1)}, u32[]{:S(2)}) copy-start(bf16[1,512,2048]{2,1,0:T(8,128)(2,1)} %all-gather.15.cloned.1.call-done) | copy-start | bytes 6291460
  140.0 454.9 %all-gather.17.cloned.1.call-start = ((), (), s32[]{:S(2)}) async-start(), calls=%async_computation.3 | async-start | bytes 18874368 | tf_op jit(solution)/shard_map/all_gather | solution.py:35
  146.5 90.4 %collective-permute-start = (bf16[2048,1024]{0,1:T(8,128)(2,1)}, bf16[2048,1024]{0,1:T(8,128)(2,1)}, u32[]{:S(2)}, u32[]{:S(2)}) collective-permute-start(bf16[2048,1024]{0,1:T(8,128)(2,1)} %bitcast.87), channel_id=1, source_target_pairs={{0,24},{8,0},{16,8},{24,16},{1,25},{9,1},{17,9},{25,17},{2,26},{10... | collective-permute-start | bytes 12582920 | tf_op jit(solution)/shard_map/ppermute | solution.py:10
  146.7 93.0 %collective-permute-start.1 = (bf16[2048,1024]{0,1:T(8,128)(2,1)}, bf16[2048,1024]{0,1:T(8,128)(2,1)}, u32[]{:S(2)}, u32[]{:S(2)}) collective-permute-start(bf16[2048,1024]{0,1:T(8,128)(2,1)} %bitcast.88), channel_id=1, source_target_pairs={{0,8},{8,16},{16,24},{24,0},{1,9},{9,17},{17,25},{25,1},{2,10},{10... | collective-permute-start | bytes 12582920 | tf_op jit(solution)/shard_map/ppermute | solution.py:10
  147.7 6.9 copy-start.1
  248.9 2.4 copy-start
  248.9 4.5 copy-start.2
  249.0 5.1 copy-start.4
  251.4 1.3 copy-start.5
  258.1 386.1 %all-gather.19.cloned.1.call-start = ((), (), s32[]{:S(2)}) async-start(), calls=%async_computation.4 | async-start | bytes 2359296 | tf_op jit(solution)/shard_map/all_gather | solution.py:25
  258.7 399.1 %collective-permute-start.2 = (bf16[2048,1024]{0,1:T(8,128)(2,1)}, bf16[2048,1024]{0,1:T(8,128)(2,1)}, u32[]{:S(2)}, u32[]{:S(2)}) collective-permute-start(bf16[2048,1024]{0,1:T(8,128)(2,1)} %bitcast.85), channel_id=1, source_target_pairs={{0,24},{8,0},{16,8},{24,16},{1,25},{9,1},{17,9},{25,17},{2,26},{10... | collective-permute-start | bytes 12582920 | tf_op jit(solution)/shard_map/ppermute | solution.py:10
  258.7 399.0 %collective-permute-start.3 = (bf16[2048,1024]{0,1:T(8,128)(2,1)}, bf16[2048,1024]{0,1:T(8,128)(2,1)}, u32[]{:S(2)}, u32[]{:S(2)}) collective-permute-start(bf16[2048,1024]{0,1:T(8,128)(2,1)} %bitcast.86), channel_id=1, source_target_pairs={{0,8},{8,16},{16,24},{24,0},{1,9},{9,17},{17,25},{25,1},{2,10},{10... | collective-permute-start | bytes 12582920 | tf_op jit(solution)/shard_map/ppermute | solution.py:10
Sparse Core Ops, SparseCore 0:
  10.1 51.7 all-gather.14
  63.5 32.9 all-gather.10
  98.1 34.4 all-gather.12
  140.1 227.2 all-gather.20
  369.4 225.4 all-gather.16
  596.9 47.2 all-gather.18
